TPU v7x, 32 devices: a whole 2x2x4 slice. The times are simulated.
32 devices in a mesh: head: 4 (over y, core), ctx: 8 (over z, x).
Axes of the slice: x: 2, y: 2, z: 4, core: 2. Of those that a mesh axis runs over, the one named last changes fastest.
Arguments:
- queries: bfloat16 [6144, 4, 1024], P('ctx', 'head'), may hold values from -200 to 200
- keys: bfloat16 [6144, 4, 128], P('ctx', 'head'), may hold values from -6 to 6
- values: bfloat16 [6144, 4, 128], P('ctx', 'head'), may hold values from -6 to 6
- span_ids: int32 [16], replicated, may hold values from 0 to 15, as said below
Outputs:
- attn_out: bfloat16 [6144, 4, 1024], P('ctx', 'head')
Inputs may be any that keep to these rules, and one draw needn't show every extreme that they name: `span_ids`: entry 2r is below 8, entry 2r + 1 equals 15 minus entry 2r, and all entries differ.
All inputs are finite; a program needn't handle non-finite values.
Results may differ from a plain program's by a relative error of at most 0.0055.
Values may be sent and summed in bfloat16 or wider, within the bound.
A program may use at most 64 MiB of HBM per device.

v0:
```python
import functools
import math

import jax
import jax.numpy as jnp
from jax import lax
from jax.experimental import pallas as pl
from jax.experimental.pallas import tpu as pltpu
from jax.sharding import PartitionSpec as P

MESH = pl.DeviceIdType.MESH
LOW, HIGH = 0, 1
TO_PARTNER, TO_NEXT, TO_PREV = 0, 1, 2
MASKED = -1e30
SLAB = 4
SLABS_PER_STEP = 1


def kernel(
    count, head_dim, ids, q_hbm, k_hbm, v_hbm, o_hbm,
    q, kv, kv_pick, acc, top, total, out, in_sem, out_sem, send_sem, recv_sem,
):
    groups, rows, _ = q.shape
    span = rows // 2
    line = count // 2
    lanes = head_dim
    slab = math.gcd(groups, SLAB)
    per_step = math.gcd(groups // slab, SLABS_PER_STEP)
    tall = slab * span
    scale = head_dim ** (-0.5) * math.log2(math.e)
    me = lax.axis_index("ctx")
    z = me // 2
    x = me % 2
    partner = z * 2 + 1 - x

    def kv_in(half, which, src):
        return pltpu.make_async_copy(
            src.at[pl.ds(half * span, span), :], kv.at[me, half, which], in_sem.at[half, which]
        )

    def q_in(group):
        return pltpu.make_async_copy(
            q_hbm.at[:, pl.ds(group * lanes, lanes)], q.at[group], in_sem.at[2 + group, 0]
        )

    for half in range(2):
        kv_in(half, 0, k_hbm).start()
        kv_in(half, 1, v_hbm).start()
    for group in range(groups):
        q_in(group).start()

    barrier = pltpu.get_barrier_semaphore()
    pl.semaphore_signal(barrier, inc=1, device_id={"ctx": partner}, device_id_type=MESH)

    @pl.when(z > 0)
    def _():
        pl.semaphore_signal(barrier, inc=1, device_id={"ctx": me - 2}, device_id_type=MESH)

    @pl.when(z < line - 1)
    def _():
        pl.semaphore_signal(barrier, inc=1, device_id={"ctx": me + 2}, device_id_type=MESH)

    near = 1 + jnp.where(z > 0, 1, 0) + jnp.where(z < line - 1, 1, 0)
    pl.semaphore_wait(barrier, near)

    def sent(owner, half, way):
        target = (partner, me + 2, me - 2)[way]
        return pltpu.make_async_remote_copy(
            src_ref=kv.at[owner, half],
            dst_ref=kv.at[owner, half],
            send_sem=send_sem.at[owner, half, way],
            recv_sem=recv_sem.at[owner, half],
            device_id={"ctx": target},
            device_id_type=MESH,
        )

    for half in range(2):
        kv_in(half, 0, k_hbm).wait()
        kv_in(half, 1, v_hbm).wait()

        @pl.when(z < line - 1)
        def _():
            sent(me, half, TO_NEXT).start()

        @pl.when(z > 0)
        def _():
            sent(me, half, TO_PREV).start()

        sent(me, half, TO_PARTNER).start()

    def relay(step, half):
        before = z - step
        after = z + step

        @pl.when(before >= 0)
        def _():
            owner = before * 2 + x
            sent(owner, half, TO_PARTNER).wait_recv()

            @pl.when(z < line - 1)
            def _():
                sent(owner, half, TO_NEXT).start()

            sent(owner, half, TO_PARTNER).start()

        @pl.when(after < line)
        def _():
            owner = after * 2 + x
            sent(owner, half, TO_PARTNER).wait_recv()

            @pl.when(z > 0)
            def _():
                sent(owner, half, TO_PREV).start()

            sent(owner, half, TO_PARTNER).start()

    for group in range(groups):
        q_in(group).wait()

    def score(q_part, k_part):
        return lax.dot_general(
            q_part, k_part, (((1,), (1,)), ((), ())), preferred_element_type=jnp.float32
        )

    def row_top(s):
        best = s[:, :lanes]
        for piece in range(1, s.shape[1] // lanes):
            best = jnp.maximum(best, s[:, piece * lanes : (piece + 1) * lanes])
        return jnp.max(best, axis=1, keepdims=True)

    def weigh(s, m):
        parts = [
            jnp.exp2((s[:, piece * lanes : (piece + 1) * lanes] - m) * scale)
            for piece in range(s.shape[1] // lanes)
        ]
        summed = parts[0]
        for part in parts[1:]:
            summed = summed + part
        return jnp.concatenate([part.astype(jnp.bfloat16) for part in parts], axis=1), summed

    def mix(p, v_part):
        return jnp.dot(p, v_part, preferred_element_type=jnp.float32)

    def over_groups(body):
        def step(index, carry):
            for inner in range(per_step):
                body(pl.ds((index * per_step + inner) * slab, slab))
            return carry

        lax.fori_loop(0, groups // (slab * per_step), step, 0)

    def half_q(group, half):
        return q[group, half * span : (half + 1) * span, :].reshape(tall, lanes)

    def read(ref, half, group):
        return ref[half, group].reshape(tall, lanes)

    def write(ref, half, group, value):
        ref[half, group] = value.reshape(slab, span, lanes)

    def own_span(half):
        row_no = lax.broadcasted_iota(jnp.int32, (tall, span), 0) % span
        key_no = lax.broadcasted_iota(jnp.int32, (tall, span), 1)

        def body(group):
            s = score(half_q(group, half), kv[me, half, 0])
            s = jnp.where(key_no <= row_no, s, MASKED)
            m = jnp.broadcast_to(row_top(s), (tall, lanes))
            p, summed = weigh(s, m)
            write(top, half, group, m)
            write(total, half, group, summed)
            write(acc, half, group, mix(p, kv[me, half, 1]))

        over_groups(body)

    def high_on_low(owners):
        def body(group):
            keys = jnp.concatenate([kv[owner, LOW, 0] for owner in owners], axis=0)
            values = jnp.concatenate([kv[owner, LOW, 1] for owner in owners], axis=0)
            s = score(half_q(group, HIGH), keys)
            old = read(top, HIGH, group)
            m = jnp.maximum(old, row_top(s))
            fade = jnp.exp2((old - m) * scale)
            p, summed = weigh(s, m)
            write(top, HIGH, group, m)
            write(total, HIGH, group, read(total, HIGH, group) * fade + summed)
            write(acc, HIGH, group, read(acc, HIGH, group) * fade + mix(p, values))

        over_groups(body)

    def one_same_half(owner):
        flag = jnp.where(ids[2 * owner] > ids[2 * me], 1, 0)
        is_high = jnp.full((tall, lanes), flag, jnp.int32) == 1
        key_high = jnp.full((span, lanes), flag, jnp.int32) == 1
        for which in range(2):
            kv_pick[which] = jnp.where(key_high, kv[owner, HIGH, which], kv[owner, LOW, which])

        def body(group):
            s = score(jnp.where(is_high, half_q(group, HIGH), half_q(group, LOW)), kv_pick[0])
            tops = [read(top, half, group) for half in range(2)]
            old = jnp.where(is_high, tops[HIGH], tops[LOW])
            m = jnp.maximum(old, row_top(s))
            fade = jnp.exp2((old - m) * scale)
            p, summed = weigh(s, m)
            write(top, LOW, group, jnp.where(is_high, tops[LOW], m))
            write(top, HIGH, group, jnp.where(is_high, m, tops[HIGH]))
            added = mix(p, kv_pick[1])
            for ref, extra in ((total, summed), (acc, added)):
                low_now, high_now = read(ref, LOW, group), read(ref, HIGH, group)
                new = jnp.where(is_high, high_now, low_now) * fade + extra
                write(ref, LOW, group, jnp.where(is_high, low_now, new))
                write(ref, HIGH, group, jnp.where(is_high, new, high_now))

        over_groups(body)

    def same_half(owners):
        def one(index, carry):
            owner = owners[0]
            for place in range(1, len(owners)):
                owner = jnp.where(index == place, owners[place], owner)
            one_same_half(owner)
            return carry

        lax.fori_loop(0, len(owners), one, 0)

    own_span(LOW)
    own_span(HIGH)
    high_on_low((me,))

    short = jnp.minimum(z, line - 1 - z)
    far_side = jnp.where(z <= line - 1 - z, 1, -1)

    def line_place(order):
        paired = jnp.where(order % 2 == 1, -1, 1) * ((order + 1) // 2)
        alone = far_side * (order - short)
        return z + jnp.where(order <= 2 * short, paired, alone)

    def arrived(owner, half):
        sent(owner, half, TO_PARTNER).wait_recv()

    def crossed(order):
        return jnp.where(order == 0, z, line_place(order)) * 2 + 1 - x

    def visit(index, carry):
        across = crossed(index)
        along = line_place(index + 1) * 2 + x
        relay(index + 1, LOW)
        arrived(across, LOW)
        high_on_low((across, along))
        relay(index + 1, HIGH)
        arrived(across, HIGH)
        same_half((across, along))
        return carry

    lax.fori_loop(0, line - 1, visit, 0)
    last = crossed(jnp.int32(line - 1))
    arrived(last, LOW)
    high_on_low((last,))
    arrived(last, HIGH)
    same_half((last,))

    def finish(group):
        for half in range(2):
            weight = jnp.sum(total[half, group], axis=1, keepdims=True)
            out[group, half * span : (half + 1) * span, :] = (
                acc[half, group] / weight
            ).astype(out.dtype)

    def result(group):
        return pltpu.make_async_copy(
            out.at[group], o_hbm.at[:, pl.ds(group * lanes, lanes)], out_sem.at[group]
        )

    for group in range(groups):
        finish(group)
        result(group).start()

    def settle(place, carry):
        owner = place * 2 + x
        for half in range(2):
            sent(owner, half, TO_PARTNER).wait_send()

            @pl.when(jnp.logical_and(place <= z, z < line - 1))
            def _():
                sent(owner, half, TO_NEXT).wait_send()

            @pl.when(jnp.logical_and(place >= z, z > 0))
            def _():
                sent(owner, half, TO_PREV).wait_send()

        return carry

    lax.fori_loop(0, line, settle, 0)
    for group in range(groups):
        result(group).wait()


def local(count, queries, keys, values, span_ids):
    rows = queries.shape[0]
    head_dim = keys.shape[2]
    width = queries.shape[2]
    groups = width // head_dim
    span = rows // 2
    any_space = pl.BlockSpec(memory_space=pl.ANY)
    out = pl.pallas_call(
        functools.partial(kernel, count, head_dim),
        out_shape=jax.ShapeDtypeStruct((rows, width), jnp.bfloat16),
        in_specs=[pl.BlockSpec(memory_space=pltpu.SMEM), any_space, any_space, any_space],
        out_specs=any_space,
        scratch_shapes=[
            pltpu.VMEM((groups, rows, head_dim), jnp.bfloat16),
            pltpu.VMEM((count, 2, 2, span, head_dim), jnp.bfloat16),
            pltpu.VMEM((2, span, head_dim), jnp.bfloat16),
            pltpu.VMEM((2, groups, span, head_dim), jnp.float32),
            pltpu.VMEM((2, groups, span, head_dim), jnp.float32),
            pltpu.VMEM((2, groups, span, head_dim), jnp.float32),
            pltpu.VMEM((groups, rows, head_dim), jnp.bfloat16),
            pltpu.SemaphoreType.DMA((2 + groups, 2)),
            pltpu.SemaphoreType.DMA((groups,)),
            pltpu.SemaphoreType.DMA((count, 2, 3)),
            pltpu.SemaphoreType.DMA((count, 2)),
        ],
        compiler_params=pltpu.CompilerParams(
            collective_id=0, has_side_effects=True, vmem_limit_bytes=56 * 2**20
        ),
    )(
        span_ids,
        queries.reshape(rows, width),
        keys.reshape(rows, head_dim),
        values.reshape(rows, head_dim),
    )
    return out.reshape(rows, 1, width)


def solution(mesh):
    in_specs = (P("ctx", "head", None), P("ctx", "head", None), P("ctx", "head", None), P())
    out_specs = P("ctx", "head", None)
    body = functools.partial(local, mesh.shape["ctx"])
    return jax.shard_map(body, mesh=mesh, in_specs=in_specs, out_specs=out_specs, check_vma=False)
```

profile of v0, /device:TPU:16, one launch (start us, length us, event | category | flops | bytes accessed | tf_op | source)
XLA Modules:
  0.0 49.6 jit_solution(14757075211580756192)
XLA Ops:
  0.0 46.9 %shard_map.46 = bf16[768,1024]{1,0:T(8,128)(2,1)} custom-call(s32[16]{0:T(128)} %ids.1, bf16[768,1024]{1,0:T(8,128)(2,1)} %bitcast.5, bf16[768,128]{1,0:T(8,128)(2,1)} %bitcast.6, bf16[768,128]{1,0:T(8,128)(2,1)} %bitcast.7), custom_call_target="tpu_custom_call" | custom-call | tf_op jit(solution)/shard_map/pallas_call | solution.py:305
  46.9 2.7 %copy.6 = bf16[768,1,1024]{2,0,1:T(8,128)(2,1)} copy(bf16[768,1,1024]{2,0,1:T(8,128)(2,1)} %bitcast.4) | data formatting | bytes 3145728
where the time goes:
time: 49.7 us; the launch traced here: 49.6 us
  Pallas kernels  46.9 us (94%)
  local copies, waits for them, and re-layouts  2.67 us (5%)
    pallas_call x1, Pallas kernels, local(): pl.pallas_call(functools.partial(kernel, count, head_dim), out_shape=jax....  46.9 us
    unnamed x1, local copies, waits for them, and re-layouts  2.67 us

commit v1 on v0

v1 whole, which is shorter than its diff:
```python
import functools
import math

import jax
import jax.numpy as jnp
from jax import lax
from jax.experimental import pallas as pl
from jax.experimental.pallas import tpu as pltpu
from jax.sharding import PartitionSpec as P

MESH = pl.DeviceIdType.MESH
LOW, HIGH = 0, 1
TO_PARTNER, TO_NEXT, TO_PREV = 0, 1, 2
MASKED = -1e30
TILE = 512
ONES = 16
EMPTY, HIGH_ON_LOW, OWN_LOW, OWN_HIGH, REMOTE = 0, 1, 2, 3, 4


def kernel(
    count, head_dim, ids, q_hbm, k_hbm, v_hbm, o_hbm,
    q_in, q, kv, acc, top, total, s_even, s_odd, p_even, p_odd, out,
    in_sem, out_sem, send_sem, recv_sem,
):
    _, wide, lanes = q_in.shape
    rows = out.shape[1]
    groups = wide * 2 // rows
    span = rows // 2
    line = count // 2
    width = s_even.shape[1]
    tiles = wide // width
    sub = top.shape[1]
    scale = head_dim ** (-0.5) * math.log2(math.e)
    me = lax.axis_index("ctx")
    z = me // 2
    x = me % 2
    partner = z * 2 + 1 - x
    first, last = 1 - x, (line - 1) * 2 + 1 - x

    def kv_in(half, which, src):
        return pltpu.make_async_copy(
            src.at[pl.ds(half * span, span), :], kv.at[me, half, which], in_sem.at[half, which]
        )

    def q_copy(group, half):
        return pltpu.make_async_copy(
            q_hbm.at[pl.ds(half * span, span), pl.ds(group * lanes, lanes)],
            q_in.at[half, pl.ds(group * span, span), :],
            in_sem.at[2 + group, half],
        )

    for half in range(2):
        kv_in(half, 0, k_hbm).start()
        kv_in(half, 1, v_hbm).start()
    for half in range(2):
        for group in range(groups):
            q_copy(group, half).start()

    barrier = pltpu.get_barrier_semaphore()
    pl.semaphore_signal(barrier, inc=1, device_id={"ctx": partner}, device_id_type=MESH)

    @pl.when(z > 0)
    def _():
        pl.semaphore_signal(barrier, inc=1, device_id={"ctx": me - 2}, device_id_type=MESH)

    @pl.when(z < line - 1)
    def _():
        pl.semaphore_signal(barrier, inc=1, device_id={"ctx": me + 2}, device_id_type=MESH)

    near = 1 + jnp.where(z > 0, 1, 0) + jnp.where(z < line - 1, 1, 0)
    pl.semaphore_wait(barrier, near)

    def sent(owner, half, way):
        target = (partner, me + 2, me - 2)[way]
        return pltpu.make_async_remote_copy(
            src_ref=kv.at[owner, half],
            dst_ref=kv.at[owner, half],
            send_sem=send_sem.at[owner, half, way],
            recv_sem=recv_sem.at[owner, half],
            device_id={"ctx": target},
            device_id_type=MESH,
        )

    for half in range(2):
        kv_in(half, 0, k_hbm).wait()
        kv_in(half, 1, v_hbm).wait()

        @pl.when(z < line - 1)
        def _():
            sent(me, half, TO_NEXT).start()

        @pl.when(z > 0)
        def _():
            sent(me, half, TO_PREV).start()

        sent(me, half, TO_PARTNER).start()

    def arrived(owner, half):
        sent(owner, half, TO_PARTNER).wait_recv()

    def crosses(place, half):
        if half == LOW:
            return place >= 0
        by_line = jnp.where(z > 0, jnp.where(place == 0, 1, 0), 0) + jnp.where(
            z < line - 1, jnp.where(place == line - 1, 1, 0), 0
        )
        return by_line == 0

    def relay(step, half):
        before = z - step
        after = z + step

        @pl.when(before >= 0)
        def _():
            owner = before * 2 + x
            arrived(owner, half)

            @pl.when(z < line - 1)
            def _():
                sent(owner, half, TO_NEXT).start()

            @pl.when(crosses(before, half))
            def _():
                sent(owner, half, TO_PARTNER).start()

        @pl.when(after < line)
        def _():
            owner = after * 2 + x
            arrived(owner, half)

            @pl.when(z > 0)
            def _():
                sent(owner, half, TO_PREV).start()

            @pl.when(crosses(after, half))
            def _():
                sent(owner, half, TO_PARTNER).start()

    def pass_on(index):
        @pl.when(index == z)
        def _():
            arrived(first, HIGH)
            sent(first, HIGH, TO_NEXT).start()

        @pl.when(index == line - 1 - z)
        def _():
            arrived(last, HIGH)
            sent(last, HIGH, TO_PREV).start()

    def split_q(group, carry):
        place = pl.ds(pl.multiple_of(group * span, span), span)
        for half in range(2):
            scaled = q_in[half, place, :].astype(jnp.float32) * scale
            coarse = scaled.astype(jnp.bfloat16)
            fine = (scaled - coarse.astype(jnp.float32)).astype(jnp.bfloat16)
            q[half, place, :] = jnp.concatenate([coarse, fine], axis=1)
        return carry

    acc[EMPTY] = jnp.zeros((lanes, wide), jnp.float32)
    top[EMPTY] = jnp.full((sub, wide), MASKED, jnp.float32)
    total[EMPTY] = jnp.zeros((sub, wide), jnp.float32)
    for half in range(2):
        for group in range(groups):
            q_copy(group, half).wait()
    lax.fori_loop(0, groups, split_q, 0)

    def job(half, key_part, value_part, source, target, masked=False):
        keys = jnp.concatenate([key_part, key_part], axis=1)
        values = jnp.concatenate(
            [value_part.T, jnp.ones((ONES, span), value_part.dtype)], axis=0
        )

        def cut(tile):
            return slice(tile * width, (tile + 1) * width)

        def score(tile):
            s = lax.dot_general(
                keys, q[half, cut(tile), :], (((1,), (1,)), ((), ())),
                preferred_element_type=jnp.float32,
            )
            if masked:
                key_no = lax.broadcasted_iota(jnp.int32, (span, width), 0)
                row_no = (lax.broadcasted_iota(jnp.int32, (span, width), 1) + tile * width) % span
                s = jnp.where(key_no <= row_no, s, MASKED)
            (s_even, s_odd)[tile % 2][...] = s
            best = s[:sub]
            for piece in range(1, span // sub):
                best = jnp.maximum(best, s[piece * sub : (piece + 1) * sub])
            old = top[source, :, cut(tile)]
            m = jnp.maximum(old, jnp.max(best, axis=0, keepdims=True))
            top[target, :, cut(tile)] = m
            return m, jnp.exp2(old - m)

        def weigh(tile, m):
            s = (s_even, s_odd)[tile % 2]
            p = (p_even, p_odd)[tile % 2]
            for piece in range(0, span, 2 * sub):
                parts = [
                    jnp.exp2(s[piece + shift : piece + shift + sub] - m) for shift in (0, sub)
                ]
                p[piece : piece + 2 * sub] = jnp.concatenate(parts, axis=0).astype(p.dtype)

        def mix(tile, fade):
            p = (p_even, p_odd)[tile % 2]
            added = jnp.dot(values, p[...], preferred_element_type=jnp.float32)
            spread = jnp.broadcast_to(fade[:1], (lanes, width))
            acc[target, :, cut(tile)] = acc[source, :, cut(tile)] * spread + added[:lanes]
            total[target, :, cut(tile)] = (
                total[source, :, cut(tile)] * fade + added[lanes : lanes + sub]
            )

        state = {}
        for tile in range(-1, tiles + 1):
            if tile + 1 < tiles:
                state[tile + 1] = score(tile + 1)
            if 0 <= tile < tiles:
                weigh(tile, state[tile][0])
            if tile >= 1:
                mix(tile - 1, state[tile - 1][1])

    def own(half, carry):
        job(half, kv[me, half, 0], kv[me, half, 1], EMPTY, OWN_LOW + half, masked=True)
        return carry

    def high_on_low(owner, source):
        job(HIGH, kv[owner, LOW, 0], kv[owner, LOW, 1], source, HIGH_ON_LOW)

    short = jnp.minimum(z, line - 1 - z)
    far_side = jnp.where(z <= line - 1 - z, 1, -1)

    def line_place(order):
        paired = jnp.where(order % 2 == 1, -1, 1) * ((order + 1) // 2)
        alone = far_side * (order - short)
        return z + jnp.where(order <= 2 * short, paired, alone)

    def crossed(order):
        return jnp.where(order == 0, z, line_place(order)) * 2 + 1 - x

    def visited(index, place):
        return jnp.where(place == 0, crossed(index), line_place(index + 1) * 2 + x)

    def is_higher(owner):
        return jnp.where(ids[2 * owner] > ids[2 * me], 1, 0)

    def chain_ends(until):
        low_end, high_end = OWN_LOW, OWN_HIGH
        for turn in range(count - 1):
            flag = is_higher(visited(turn // 2, turn % 2))
            counts = jnp.where(turn < until, 1, 0)
            low_end = jnp.where(counts * (1 - flag) == 1, REMOTE + turn, low_end)
            high_end = jnp.where(counts * flag == 1, REMOTE + turn, high_end)
        return low_end, high_end

    def same_half(owner, turn):
        flag = is_higher(owner)
        is_high = jnp.full((span, lanes), flag, jnp.int32) == 1
        key_part, value_part = [
            jnp.where(is_high, kv[owner, HIGH, which], kv[owner, LOW, which]) for which in range(2)
        ]
        low_end, high_end = chain_ends(turn)
        job(flag, key_part, value_part, jnp.where(flag == 1, high_end, low_end), REMOTE + turn)

    lax.fori_loop(0, 2, own, 0)

    def visit(index, carry):
        across = jnp.where(index < 0, me, crossed(jnp.maximum(index, 0)))
        along = line_place(index + 1) * 2 + x
        some = jnp.logical_and(index >= 0, index < line - 1)
        both = jnp.where(some, 2, 1)

        @pl.when(some)
        def _():
            relay(index + 1, LOW)

        @pl.when(index >= 0)
        def _():
            arrived(across, LOW)

        def low_one(place, carry):
            owner = jnp.where(place == 0, across, along)
            high_on_low(owner, jnp.where(index < 0, EMPTY, HIGH_ON_LOW))
            return carry

        lax.fori_loop(0, both, low_one, 0)

        @pl.when(some)
        def _():
            relay(index + 1, HIGH)
            pass_on(index)

        @pl.when(index >= 0)
        def _():
            arrived_high(index, across)

        def same_one(place, carry):
            owner = jnp.where(place == 0, across, along)
            same_half(owner, 2 * index + place)
            return carry

        lax.fori_loop(0, jnp.where(index < 0, 0, both), same_one, 0)
        return carry

    def arrived_high(index, across):
        from_first = jnp.where(z < line - 1, jnp.where(across == first, 1, 0), 0)
        from_last = jnp.where(z > 0, jnp.where(across == last, 1, 0), 0)
        taken = from_first * jnp.where(index >= z, 1, 0) + from_last * jnp.where(
            index >= line - 1 - z, 1, 0
        )

        @pl.when(taken == 0)
        def _():
            arrived(across, HIGH)

    lax.fori_loop(-1, line, visit, 0)
    low_end, high_end = chain_ends(count - 1)

    def finish(group):
        part = slice(group * span, (group + 1) * span)
        weight = 1.0 / total[low_end, :, part]
        mixed = acc[low_end, :, part] * weight[:1]
        out[group, :span, :] = mixed.astype(out.dtype).T
        m = jnp.maximum(top[HIGH_ON_LOW, :, part], top[high_end, :, part])
        fades = [jnp.exp2(top[which, :, part] - m) for which in (HIGH_ON_LOW, high_end)]
        weight = 1.0 / (
            total[HIGH_ON_LOW, :, part] * fades[0] + total[high_end, :, part] * fades[1]
        )
        mixed = acc[HIGH_ON_LOW, :, part] * (fades[0] * weight)[:1]
        mixed = mixed + acc[high_end, :, part] * (fades[1] * weight)[:1]
        out[group, span:, :] = mixed.astype(out.dtype).T

    def result(group):
        return pltpu.make_async_copy(
            out.at[group], o_hbm.at[:, pl.ds(group * lanes, lanes)], out_sem.at[group]
        )

    for group in range(groups):
        finish(group)
        result(group).start()

    def settle(place, carry):
        owner = place * 2 + x
        for half in range(2):
            @pl.when(crosses(place, half))
            def _():
                sent(owner, half, TO_PARTNER).wait_send()

            @pl.when(jnp.logical_and(place <= z, z < line - 1))
            def _():
                sent(owner, half, TO_NEXT).wait_send()

            @pl.when(jnp.logical_and(place >= z, z > 0))
            def _():
                sent(owner, half, TO_PREV).wait_send()

        return carry

    lax.fori_loop(0, line, settle, 0)

    @pl.when(z < line - 1)
    def _():
        sent(first, HIGH, TO_NEXT).wait_send()

    @pl.when(z > 0)
    def _():
        sent(last, HIGH, TO_PREV).wait_send()

    for group in range(groups):
        result(group).wait()


def local(count, queries, keys, values, span_ids):
    rows = queries.shape[0]
    head_dim = keys.shape[2]
    width = queries.shape[2]
    groups = width // head_dim
    span = rows // 2
    wide = groups * span
    tile = math.gcd(wide, TILE)
    states = REMOTE + count - 1
    any_space = pl.BlockSpec(memory_space=pl.ANY)
    out = pl.pallas_call(
        functools.partial(kernel, count, head_dim),
        out_shape=jax.ShapeDtypeStruct((rows, width), jnp.bfloat16),
        in_specs=[pl.BlockSpec(memory_space=pltpu.SMEM), any_space, any_space, any_space],
        out_specs=any_space,
        scratch_shapes=[
            pltpu.VMEM((2, wide, head_dim), jnp.bfloat16),
            pltpu.VMEM((2, wide, 2 * head_dim), jnp.bfloat16),
            pltpu.VMEM((count, 2, 2, span, head_dim), jnp.bfloat16),
            pltpu.VMEM((states, head_dim, wide), jnp.float32),
            pltpu.VMEM((states, 8, wide), jnp.float32),
            pltpu.VMEM((states, 8, wide), jnp.float32),
            pltpu.VMEM((span, tile), jnp.float32),
            pltpu.VMEM((span, tile), jnp.float32),
            pltpu.VMEM((span, tile), jnp.bfloat16),
            pltpu.VMEM((span, tile), jnp.bfloat16),
            pltpu.VMEM((groups, rows, head_dim), jnp.bfloat16),
            pltpu.SemaphoreType.DMA((2 + groups, 2)),
            pltpu.SemaphoreType.DMA((groups,)),
            pltpu.SemaphoreType.DMA((count, 2, 3)),
            pltpu.SemaphoreType.DMA((count, 2)),
        ],
        compiler_params=pltpu.CompilerParams(
            collective_id=0, has_side_effects=True, vmem_limit_bytes=56 * 2**20
        ),
    )(
        span_ids,
        queries.reshape(rows, width),
        keys.reshape(rows, head_dim),
        values.reshape(rows, head_dim),
    )
    return out.reshape(rows, 1, width)


def solution(mesh):
    in_specs = (P("ctx", "head", None), P("ctx", "head", None), P("ctx", "head", None), P())
    out_specs = P("ctx", "head", None)
    body = functools.partial(local, mesh.shape["ctx"])
    return jax.shard_map(body, mesh=mesh, in_specs=in_specs, out_specs=out_specs, check_vma=False)
```

time: 49.7 us -> 46.2 us (0.930)
  Pallas kernels: 46.9 us -> 43.4 us
    pallas_call x1, Pallas kernels: 46.9 us -> 43.4 us  [local(): pl.pallas_call(functools.partial(kernel, count, head_dim), out_shape=jax....]
where the time goes in v1:
time: 46.2 us; the launch traced here: 46.1 us
  Pallas kernels  43.4 us (94%)
  local copies, waits for them, and re-layouts  2.67 us (6%)
    pallas_call x1, Pallas kernels, local(): pl.pallas_call(functools.partial(kernel, count, head_dim), out_shape=jax....  43.4 us
    unnamed x1, local copies, waits for them, and re-layouts  2.67 us

profile of v1, /device:TPU:16, one launch (start us, length us, event | category | flops | bytes accessed | tf_op | source)
XLA Modules:
  0.0 46.1 jit_solution(9927225784158735657)
XLA Ops:
  0.0 43.4 %shard_map.46 = bf16[768,1024]{1,0:T(8,128)(2,1)} custom-call(s32[16]{0:T(128)} %ids.1, bf16[768,1024]{1,0:T(8,128)(2,1)} %bitcast.5, bf16[768,128]{1,0:T(8,128)(2,1)} %bitcast.6, bf16[768,128]{1,0:T(8,128)(2,1)} %bitcast.7), custom_call_target="tpu_custom_call" | custom-call | tf_op jit(solution)/shard_map/pallas_call | solution.py:381
  43.4 2.7 %copy.6 = bf16[768,1,1024]{2,0,1:T(8,128)(2,1)} copy(bf16[768,1,1024]{2,0,1:T(8,128)(2,1)} %bitcast.4) | data formatting | bytes 3145728

commit v2 on v1

v2 whole, which is shorter than its diff:
```python
import functools
import math

import jax
import jax.numpy as jnp
from jax import lax
from jax.experimental import pallas as pl
from jax.experimental.pallas import tpu as pltpu
from jax.sharding import PartitionSpec as P

MESH = pl.DeviceIdType.MESH
LOW, HIGH = 0, 1
PIECES = 2
TO_PARTNER, TO_NEXT, TO_PREV = 0, 1, 2
MASKED = -1e30
TILE = 512
ONES = 16
EMPTY, HIGH_ON_LOW, OWN_LOW, OWN_HIGH, REMOTE = 0, 1, 2, 3, 4


def kernel(
    count, head_dim, ids, q_hbm, k_hbm, v_hbm, out,
    q_in, q, kv, acc, top, total, s_even, s_odd, p_even, p_odd,
    kv_sem, in_sem, send_sem, recv_sem,
):
    _, wide, lanes = q_in.shape
    rows = out.shape[0]
    groups = wide * 2 // rows
    span = rows // 2
    line = count // 2
    width = s_even.shape[1]
    tiles = wide // width
    sub = top.shape[1]
    scale = head_dim ** (-0.5) * math.log2(math.e)
    me = lax.axis_index("ctx")
    z = me // 2
    x = me % 2
    partner = z * 2 + 1 - x
    first, last = 1 - x, (line - 1) * 2 + 1 - x
    near_end = jnp.where(z <= line - 1 - z, -1, 1)

    short_span = span // PIECES

    def kv_in(half, piece, which):
        return pltpu.make_async_copy(
            (k_hbm, v_hbm)[which].at[pl.ds(half * span + piece * short_span, short_span), :],
            kv.at[me, half, piece, which],
            kv_sem.at[half, piece, which],
        )

    def q_copy(group, half):
        return pltpu.make_async_copy(
            q_hbm.at[pl.ds(half * span, span), pl.ds(group * lanes, lanes)],
            q_in.at[half, pl.ds(group * span, span), :],
            in_sem.at[group, half],
        )

    for half in range(2):
        for piece in range(PIECES):
            for which in range(2):
                kv_in(half, piece, which).start()
    for half in range(2):
        for group in range(groups):
            q_copy(group, half).start()

    barrier = pltpu.get_barrier_semaphore()
    pl.semaphore_signal(barrier, inc=1, device_id={"ctx": partner}, device_id_type=MESH)

    @pl.when(z > 0)
    def _():
        pl.semaphore_signal(barrier, inc=1, device_id={"ctx": me - 2}, device_id_type=MESH)

    @pl.when(z < line - 1)
    def _():
        pl.semaphore_signal(barrier, inc=1, device_id={"ctx": me + 2}, device_id_type=MESH)

    near = 1 + jnp.where(z > 0, 1, 0) + jnp.where(z < line - 1, 1, 0)
    pl.semaphore_wait(barrier, near)

    def piece_sent(owner, half, piece, way):
        along = jnp.where(way == TO_NEXT, me + 2, me - 2)
        target = jnp.where(way == TO_PARTNER, partner, along)
        return pltpu.make_async_remote_copy(
            src_ref=kv.at[owner, half, piece],
            dst_ref=kv.at[owner, half, piece],
            send_sem=send_sem.at[owner, half, piece, way],
            recv_sem=recv_sem.at[owner, half, piece],
            device_id={"ctx": target},
            device_id_type=MESH,
        )

    class Sent:
        def __init__(self, owner, half, way):
            self.copies = [piece_sent(owner, half, piece, way) for piece in range(PIECES)]

        def start(self):
            for copy in self.copies:
                copy.start()

        def wait_send(self):
            for copy in self.copies:
                copy.wait_send()

        def wait_recv(self):
            for copy in self.copies:
                copy.wait_recv()

    sent = Sent

    for half in range(2):
        for piece in range(PIECES):
            for which in range(2):
                kv_in(half, piece, which).wait()

            @pl.when(z < line - 1)
            def _():
                piece_sent(me, half, piece, TO_NEXT).start()

            @pl.when(z > 0)
            def _():
                piece_sent(me, half, piece, TO_PREV).start()

            piece_sent(me, half, piece, TO_PARTNER).start()

    def arrived(owner, half, pieces=range(PIECES)):
        for piece in pieces:
            piece_sent(owner, half, piece, TO_PARTNER).wait_recv()

    def crosses(place, half):
        if half == LOW:
            return place >= 0
        by_line = jnp.where(z > 0, jnp.where(place == 0, 1, 0), 0) + jnp.where(
            z < line - 1, jnp.where(place == line - 1, 1, 0), 0
        )
        return by_line == 0

    def relay(step, half):
        for place in (z + near_end * step, z - near_end * step):
            inside = jnp.where(place >= 0, 1, 0) * jnp.where(place < line, 1, 0)
            onward = jnp.where(place < z, jnp.where(z < line - 1, 1, 0), jnp.where(z > 0, 1, 0))
            owner = place * 2 + x

            @pl.when(inside == 1)
            def _():
                arrived(owner, half)

            @pl.when(inside * onward == 1)
            def _():
                sent(owner, half, jnp.where(place < z, TO_NEXT, TO_PREV)).start()

            @pl.when(jnp.logical_and(inside == 1, crosses(place, half)))
            def _():
                sent(owner, half, TO_PARTNER).start()

    def pass_on(index):
        @pl.when(index == z)
        def _():
            arrived(first, HIGH)
            sent(first, HIGH, TO_NEXT).start()

        @pl.when(index == line - 1 - z)
        def _():
            arrived(last, HIGH)
            sent(last, HIGH, TO_PREV).start()

    def split_q(group, carry):
        place = pl.ds(pl.multiple_of(group * span, span), span)
        for half in range(2):
            scaled = q_in[half, place, :].astype(jnp.float32) * scale
            coarse = scaled.astype(jnp.bfloat16)
            fine = (scaled - coarse.astype(jnp.float32)).astype(jnp.bfloat16)
            q[half, place, :] = jnp.concatenate([coarse, fine], axis=1)
        return carry

    acc[EMPTY] = jnp.zeros((lanes, wide), jnp.float32)
    top[EMPTY] = jnp.full((sub, wide), MASKED, jnp.float32)
    total[EMPTY] = jnp.zeros((sub, wide), jnp.float32)
    for half in range(2):
        for group in range(groups):
            q_copy(group, half).wait()
    lax.fori_loop(0, groups, split_q, 0)

    def cut(tile):
        return slice(tile * width, (tile + 1) * width)

    class Job:
        def __init__(self, half, key_parts, value_parts, source, target, masked=False):
            self.half, self.source, self.target, self.masked = half, source, target, masked
            keys = jnp.concatenate(key_parts, axis=0)
            self.keys = jnp.concatenate([keys, keys], axis=1)
            self.length = keys.shape[0]
            values = jnp.concatenate([part.T for part in value_parts], axis=1)
            self.values = jnp.concatenate(
                [values, jnp.ones((ONES, self.length), values.dtype)], axis=0
            )

        def score(self, tile, s_ref):
            s = lax.dot_general(
                self.keys, q[self.half, cut(tile), :], (((1,), (1,)), ((), ())),
                preferred_element_type=jnp.float32,
            )
            if self.masked:
                s = jnp.concatenate(
                    [self.causal(s, tile, place) for place in range(0, width, lanes)], axis=1
                )
            s_ref[: self.length] = s
            best = s[:sub]
            for piece in range(1, self.length // sub):
                best = jnp.maximum(best, s[piece * sub : (piece + 1) * sub])
            old = top[self.source, :, cut(tile)]
            m = jnp.maximum(old, jnp.max(best, axis=0, keepdims=True))
            top[self.target, :, cut(tile)] = m
            return m, jnp.exp2(old - m)

        def causal(self, s, tile, place):
            first_row = (tile * width + place) % span
            blocks = []
            for first_key in range(0, span, lanes):
                block = s[first_key : first_key + lanes, place : place + lanes]
                if first_key > first_row:
                    block = jnp.full_like(block, MASKED)
                elif first_key == first_row:
                    key_no = lax.broadcasted_iota(jnp.int32, block.shape, 0)
                    row_no = lax.broadcasted_iota(jnp.int32, block.shape, 1)
                    block = jnp.where(key_no <= row_no, block, MASKED)
                blocks.append(block)
            return jnp.concatenate(blocks, axis=0)

        def weigh(self, m, s, p):
            for piece in range(0, self.length, 2 * sub):
                parts = [
                    jnp.exp2(s[piece + shift : piece + shift + sub] - m) for shift in (0, sub)
                ]
                p[piece : piece + 2 * sub] = jnp.concatenate(parts, axis=0).astype(p.dtype)

        def mix(self, tile, fade, p):
            added = jnp.dot(self.values, p[: self.length], preferred_element_type=jnp.float32)
            spread = jnp.broadcast_to(fade[:1], (lanes, width))
            acc[self.target, :, cut(tile)] = (
                acc[self.source, :, cut(tile)] * spread + added[:lanes]
            )
            total[self.target, :, cut(tile)] = (
                total[self.source, :, cut(tile)] * fade + added[lanes : lanes + sub]
            )

    def run(*jobs):
        steps = [(job, tile) for job in jobs for tile in range(tiles)]
        scores, shares = (s_even, s_odd), (p_even, p_odd)
        state = {}
        for at in range(-1, len(steps) + 1):
            if at + 1 < len(steps):
                job, tile = steps[at + 1]
                state[at + 1] = job.score(tile, scores[(at + 1) % 2])
            if 0 <= at < len(steps):
                steps[at][0].weigh(state[at][0], scores[at % 2], shares[at % 2])
            if at >= 1:
                job, tile = steps[at - 1]
                job.mix(tile, state[at - 1][1], shares[(at - 1) % 2])

    every = tuple(range(PIECES))

    def parts(owner, half, which, pieces=every):
        return [kv[owner, half, piece, which] for piece in pieces]

    def own_job(half):
        return Job(
            half, parts(me, half, 0), parts(me, half, 1), EMPTY, OWN_LOW + half, masked=True
        )

    def low_job(owners, source, pieces=every):
        return Job(
            HIGH,
            [part for owner in owners for part in parts(owner, LOW, 0, pieces)],
            [part for owner in owners for part in parts(owner, LOW, 1, pieces)],
            source, HIGH_ON_LOW,
        )

    short = jnp.minimum(z, line - 1 - z)

    def line_place(order):
        paired = jnp.where(order % 2 == 1, 1, -1) * ((order + 1) // 2)
        alone = short - order
        return z + near_end * jnp.where(order <= 2 * short, paired, alone)

    def crossed(order):
        return jnp.where(order == 0, z, line_place(order)) * 2 + 1 - x

    def visited(index, place):
        return jnp.where(place == 0, crossed(index), line_place(index + 1) * 2 + x)

    def is_higher(owner):
        return jnp.where(ids[2 * owner] > ids[2 * me], 1, 0)

    def chain_ends(until):
        low_end, high_end = OWN_LOW, OWN_HIGH
        for turn in range(count - 1):
            flag = is_higher(visited(turn // 2, turn % 2))
            counts = jnp.where(turn < until, 1, 0)
            low_end = jnp.where(counts * (1 - flag) == 1, REMOTE + turn, low_end)
            high_end = jnp.where(counts * flag == 1, REMOTE + turn, high_end)
        return low_end, high_end

    def same_job(owner, turn, pieces=every, again=False):
        flag = is_higher(owner)
        is_high = jnp.full((short_span, lanes), flag, jnp.int32) == 1
        key_parts, value_parts = [
            [
                jnp.where(is_high, high, low)
                for high, low in zip(
                    parts(owner, HIGH, which, pieces), parts(owner, LOW, which, pieces)
                )
            ]
            for which in range(2)
        ]
        low_end, high_end = chain_ends(turn)
        source = REMOTE + turn if again else jnp.where(flag == 1, high_end, low_end)
        return Job(flag, key_parts, value_parts, source, REMOTE + turn)

    run(own_job(LOW), own_job(HIGH), low_job([me], EMPTY))

    def visit(index, carry):
        across, along = visited(index, 0), visited(index, 1)
        relay(index + 1, LOW)
        arrived(across, LOW)
        run(low_job([across, along], HIGH_ON_LOW))
        relay(index + 1, HIGH)
        pass_on(index)
        arrived_high(index, across)
        run(same_job(across, 2 * index), same_job(along, 2 * index + 1))
        return carry

    def arrived_high(index, across, pieces=range(PIECES)):
        from_first = jnp.where(z < line - 1, jnp.where(across == first, 1, 0), 0)
        from_last = jnp.where(z > 0, jnp.where(across == last, 1, 0), 0)
        taken = from_first * jnp.where(index >= z, 1, 0) + from_last * jnp.where(
            index >= line - 1 - z, 1, 0
        )

        @pl.when(taken == 0)
        def _():
            arrived(across, HIGH, pieces)

    lax.fori_loop(0, line - 1, visit, 0)
    final = visited(line - 1, 0)
    for piece in range(PIECES):
        arrived(final, LOW, (piece,))
        arrived_high(line - 1, final, (piece,))
        run(
            low_job([final], HIGH_ON_LOW, (piece,)),
            same_job(final, count - 2, (piece,), again=piece > 0),
        )
    low_end, high_end = chain_ends(count - 1)

    def finish(group):
        part = slice(group * span, (group + 1) * span)
        weight = 1.0 / total[low_end, :, part]
        mixed = acc[low_end, :, part] * weight[:1]
        out[:span, group * lanes : (group + 1) * lanes] = mixed.astype(out.dtype).T
        m = jnp.maximum(top[HIGH_ON_LOW, :, part], top[high_end, :, part])
        fades = [jnp.exp2(top[which, :, part] - m) for which in (HIGH_ON_LOW, high_end)]
        weight = 1.0 / (
            total[HIGH_ON_LOW, :, part] * fades[0] + total[high_end, :, part] * fades[1]
        )
        mixed = acc[HIGH_ON_LOW, :, part] * (fades[0] * weight)[:1]
        mixed = mixed + acc[high_end, :, part] * (fades[1] * weight)[:1]
        out[span:, group * lanes : (group + 1) * lanes] = mixed.astype(out.dtype).T

    for group in range(groups):
        finish(group)

    def settle(place, carry):
        owner = place * 2 + x
        for half in range(2):
            @pl.when(crosses(place, half))
            def _():
                sent(owner, half, TO_PARTNER).wait_send()

            @pl.when(jnp.logical_and(place <= z, z < line - 1))
            def _():
                sent(owner, half, TO_NEXT).wait_send()

            @pl.when(jnp.logical_and(place >= z, z > 0))
            def _():
                sent(owner, half, TO_PREV).wait_send()

        return carry

    lax.fori_loop(0, line, settle, 0)

    @pl.when(z < line - 1)
    def _():
        sent(first, HIGH, TO_NEXT).wait_send()

    @pl.when(z > 0)
    def _():
        sent(last, HIGH, TO_PREV).wait_send()


def local(count, queries, keys, values, span_ids):
    rows = queries.shape[0]
    head_dim = keys.shape[2]
    width = queries.shape[2]
    groups = width // head_dim
    span = rows // 2
    wide = groups * span
    tile = math.gcd(wide, TILE)
    states = REMOTE + count - 1
    in_hbm = pl.BlockSpec(memory_space=pltpu.HBM)
    out = pl.pallas_call(
        functools.partial(kernel, count, head_dim),
        out_shape=pltpu.VMEM((rows, width), jnp.bfloat16),
        in_specs=[pl.BlockSpec(memory_space=pltpu.SMEM), in_hbm, in_hbm, in_hbm],
        out_specs=pl.BlockSpec(memory_space=pltpu.VMEM),
        scratch_shapes=[
            pltpu.VMEM((2, wide, head_dim), jnp.bfloat16),
            pltpu.VMEM((2, wide, 2 * head_dim), jnp.bfloat16),
            pltpu.VMEM((count, 2, PIECES, 2, span // PIECES, head_dim), jnp.bfloat16),
            pltpu.VMEM((states, head_dim, wide), jnp.float32),
            pltpu.VMEM((states, 8, wide), jnp.float32),
            pltpu.VMEM((states, 8, wide), jnp.float32),
            pltpu.VMEM((rows, tile), jnp.float32),
            pltpu.VMEM((rows, tile), jnp.float32),
            pltpu.VMEM((rows, tile), jnp.bfloat16),
            pltpu.VMEM((rows, tile), jnp.bfloat16),
            pltpu.SemaphoreType.DMA((2, PIECES, 2)),
            pltpu.SemaphoreType.DMA((groups, 2)),
            pltpu.SemaphoreType.DMA((count, 2, PIECES, 3)),
            pltpu.SemaphoreType.DMA((count, 2, PIECES)),
        ],
        compiler_params=pltpu.CompilerParams(
            collective_id=0, has_side_effects=True, vmem_limit_bytes=60 * 2**20
        ),
    )(
        span_ids,
        queries.reshape(rows, width),
        keys.reshape(rows, head_dim),
        values.reshape(rows, head_dim),
    )
    return out.reshape(rows, 1, width)


def solution(mesh):
    in_specs = (P("ctx", "head", None), P("ctx", "head", None), P("ctx", "head", None), P())
    out_specs = P("ctx", "head", None)
    body = functools.partial(local, mesh.shape["ctx"])
    return jax.shard_map(body, mesh=mesh, in_specs=in_specs, out_specs=out_specs, check_vma=False)
```

time: 46.2 us -> 43.2 us (0.935)
  the two profiles are of different devices: /device:TPU:16 before, /device:TPU:0 now
where the time goes in v2:
time: 43.2 us; the launch traced here: 43.1 us
  Pallas kernels  41.9 us (97%)
  local copies, waits for them, and re-layouts  1.15 us (3%)
    pallas_call x1, Pallas kernels, local(): pl.pallas_call(functools.partial(kernel, count, head_dim), out_shape=pltp...  41.9 us
    unnamed x1, local copies, waits for them, and re-layouts  1.15 us

profile of v2, /device:TPU:0, one launch (start us, length us, event | category | flops | bytes accessed | tf_op | source)
XLA Modules:
  0.0 43.1 jit_solution(15423148670513245490)
XLA Ops:
  0.0 41.9 %shard_map.46 = bf16[768,1024]{1,0:T(8,128)(2,1)S(1)} custom-call(s32[16]{0:T(128)} %ids.1, bf16[768,1024]{1,0:T(8,128)(2,1)} %bitcast.5, bf16[768,128]{1,0:T(8,128)(2,1)} %bitcast.6, bf16[768,128]{1,0:T(8,128)(2,1)} %bitcast.7), custom_call_target="tpu_custom_call" | custom-call | tf_op jit(solution)/shard_map/pallas_call | solution.py:409
  41.9 1.1 %copy.6 = bf16[768,1,1024]{2,0,1:T(8,128)(2,1)} copy(bf16[768,1,1024]{2,0,1:T(8,128)(2,1)S(1)} %bitcast.4) | data formatting | bytes 3145728

commit v3 on v2

--- a/solution.py
+++ b/solution.py
@@ -13,7 +13,7 @@
 PIECES = 2
 TO_PARTNER, TO_NEXT, TO_PREV = 0, 1, 2
 MASKED = -1e30
-TILE = 512
+TILE = 768
 ONES = 16
 EMPTY, HIGH_ON_LOW, OWN_LOW, OWN_HIGH, REMOTE = 0, 1, 2, 3, 4
 
@@ -59,10 +59,6 @@
         for piece in range(PIECES):
             for which in range(2):
                 kv_in(half, piece, which).start()
-    for half in range(2):
-        for group in range(groups):
-            q_copy(group, half).start()
-
     barrier = pltpu.get_barrier_semaphore()
     pl.semaphore_signal(barrier, inc=1, device_id={"ctx": partner}, device_id_type=MESH)
 
@@ -122,6 +118,10 @@
 
             piece_sent(me, half, piece, TO_PARTNER).start()
 
+    for half in range(2):
+        for group in range(groups):
+            q_copy(group, half).start()
+
     def arrived(owner, half, pieces=range(PIECES)):
         for piece in pieces:
             piece_sent(owner, half, piece, TO_PARTNER).wait_recv()
@@ -152,13 +152,18 @@
             def _():
                 sent(owner, half, TO_PARTNER).start()
 
-    def pass_on(index):
-        @pl.when(index == z)
+    def pass_on(index, at_high):
+        upward = jnp.where(z == 0, 1, 0)
+        downward = jnp.where(z == line - 1, 1, 0)
+
+        @pl.when(jnp.where(index == z, 1, 0) * jnp.where(upward == at_high, 1, 0) == 1)
         def _():
             arrived(first, HIGH)
             sent(first, HIGH, TO_NEXT).start()
 
-        @pl.when(index == line - 1 - z)
+        @pl.when(
+            jnp.where(index == line - 1 - z, 1, 0) * jnp.where(downward == at_high, 1, 0) == 1
+        )
         def _():
             arrived(last, HIGH)
             sent(last, HIGH, TO_PREV).start()
@@ -321,10 +326,11 @@
     def visit(index, carry):
         across, along = visited(index, 0), visited(index, 1)
         relay(index + 1, LOW)
+        pass_on(index, 0)
         arrived(across, LOW)
         run(low_job([across, along], HIGH_ON_LOW))
         relay(index + 1, HIGH)
-        pass_on(index)
+        pass_on(index, 1)
         arrived_high(index, across)
         run(same_job(across, 2 * index), same_job(along, 2 * index + 1))
         return carry

time: 43.2 us -> 42.8 us (level)
    pallas_call x1, Pallas kernels: 41.9 us -> 41.5 us  [local(): pl.pallas_call(functools.partial(kernel, count, head_dim), out_shape=pltp...]
where the time goes in v3:
time: 42.8 us; the launch traced here: 42.6 us
  Pallas kernels  41.5 us (97%)
  local copies, waits for them, and re-layouts  1.15 us (3%)
    pallas_call x1, Pallas kernels, local(): pl.pallas_call(functools.partial(kernel, count, head_dim), out_shape=pltp...  41.5 us
    unnamed x1, local copies, waits for them, and re-layouts  1.15 us

profile of v3, /device:TPU:0, one launch (start us, length us, event | category | flops | bytes accessed | tf_op | source)
XLA Modules:
  0.0 42.6 jit_solution(17638666708782215385)
XLA Ops:
  0.0 41.5 %shard_map.46 = bf16[768,1024]{1,0:T(8,128)(2,1)S(1)} custom-call(s32[16]{0:T(128)} %ids.1, bf16[768,1024]{1,0:T(8,128)(2,1)} %bitcast.5, bf16[768,128]{1,0:T(8,128)(2,1)} %bitcast.6, bf16[768,128]{1,0:T(8,128)(2,1)} %bitcast.7), custom_call_target="tpu_custom_call" | custom-call | tf_op jit(solution)/shard_map/pallas_call | solution.py:415
  41.5 1.1 %copy.6 = bf16[768,1,1024]{2,0,1:T(8,128)(2,1)} copy(bf16[768,1,1024]{2,0,1:T(8,128)(2,1)S(1)} %bitcast.4) | data formatting | bytes 3145728
